TPU v7x, 32 devices: a whole 2x2x4 slice. The times are simulated.
32 devices in a mesh: af: 4 (over z), gx: 2 (over x), gy: 4 (over y, core).
Axes of the slice: x: 2, y: 2, z: 4, core: 2. Of those that a mesh axis runs over, the one named last changes fastest.
Arguments:
- source: float32 [4, 2048, 2048], P('af', ('gx', 'gy')), parts along dimension 0, may hold values from -0.8 to 0.8
- screening: float32 [4], P('af'), parts along dimension 0, may hold values from 0.0002 to 0.002
Outputs:
- solution: float32 [4, 2048, 2048], P('af', ('gx', 'gy')), parts along dimension 0
There are 4 independent parts, one for each index of `af`. A program takes and returns all parts, laid end to end along the dimension named above; each array names one. Nothing has to cross between parts.
All inputs are finite; a program needn't handle non-finite values.
Results may differ from a plain program's by a relative error of at most 0.0014.
Values sent between devices are 32-bit elements; how exact they have to be, the bound alone decides.
A program may use at most 128 MiB of HBM per device.

v0:
```python
import math

import jax
import jax.numpy as jnp
from jax import lax
from jax.sharding import PartitionSpec as P

HIGHEST = lax.Precision.HIGHEST


def shifted(shard, axis, by):
    devices = lax.axis_size(axis)
    pairs = [(i, i + by) for i in range(devices) if 0 <= i + by < devices]
    return lax.ppermute(shard, axis, pairs)


def sine_table(length):
    numbers = jnp.arange(length, dtype=jnp.int32) + 1
    phases = numbers[:, None] * numbers[None, :] % (2 * length + 2)
    return math.sqrt(2.0 / (length + 1)) * jnp.sin(
        phases.astype(jnp.float32) * (math.pi / (length + 1))
    )


def diagonal_factor(screening, length):
    numbers = (jnp.arange(length, dtype=jnp.int32) + 1).astype(jnp.float32)
    return 4.0 + screening[:, None] - 2.0 * jnp.cos(numbers * (math.pi / (length + 1)))[None, :]


def shift_rows(values, offset, fill_value):
    row_count = values.shape[-2]
    pad_shape = values.shape[:-2] + (abs(offset), values.shape[-1])
    padding = jnp.full(pad_shape, fill_value, values.dtype)
    if offset > 0:
        return jnp.concatenate([padding, values[..., : row_count - offset, :]], axis=-2)
    return jnp.concatenate([values[..., -offset:, :], padding], axis=-2)


def cyclic_solve(low_band, middle, up_band, all_sides):
    row_count = middle.shape[-2]
    stride = 1
    while stride < row_count:
        left_ratio = low_band / shift_rows(middle, stride, 1.0)
        right_ratio = up_band / shift_rows(middle, -stride, 1.0)
        next_low = -left_ratio * shift_rows(low_band, stride, 0.0)
        next_up = -right_ratio * shift_rows(up_band, -stride, 0.0)
        middle = (
            middle
            - left_ratio * shift_rows(up_band, stride, 0.0)
            - right_ratio * shift_rows(low_band, -stride, 0.0)
        )
        all_sides = tuple(
            (
                each_side
                - left_ratio * shift_rows(each_side, stride, 0.0)
                - right_ratio * shift_rows(each_side, -stride, 0.0)
                for each_side in all_sides
            )
        )
        low_band, up_band = (next_low, next_up)
        stride *= 2
    return tuple((each_side / middle for each_side in all_sides))


def to_lines(values):
    return lax.all_to_all(values, ("gx", "gy"), split_axis=2, concat_axis=1, tiled=True)


def to_rows(values):
    return lax.all_to_all(values, ("gx", "gy"), split_axis=1, concat_axis=2, tiled=True)


def solve_lines(reduced, center):
    groups = lax.axis_size(("gx", "gy"))
    fields, kept_lines, span_x = reduced.shape
    inner_lines = kept_lines - 1
    band_shape = (fields, inner_lines, span_x)
    row_index = lax.broadcasted_iota(jnp.int32, band_shape, 1)
    low_band = jnp.where(row_index > 0, -1.0, 0.0)
    up_band = jnp.where(row_index < inner_lines - 1, -1.0, 0.0)
    middle = jnp.broadcast_to(center, band_shape)
    first_unit = jnp.where(row_index == 0, 1.0, 0.0)
    last_unit = jnp.where(row_index == inner_lines - 1, 1.0, 0.0)
    base_part, left_spike, right_spike = cyclic_solve(
        low_band, middle, up_band, (reduced[:, :inner_lines, :], first_unit, last_unit)
    )
    separator_side = reduced[:, inner_lines:, :] + base_part[:, inner_lines - 1 :, :]
    head_value = base_part[:, :1, :]
    sides_all, heads_all = (
        lax.all_gather(separator_side, ("gx", "gy"), axis=1, tiled=True),
        lax.all_gather(head_value, ("gx", "gy"), axis=1, tiled=True),
    )
    later_heads = jnp.concatenate(
        [heads_all[:, 1:, :], jnp.zeros_like(heads_all[:, :1, :])], axis=1
    )
    chain_side = sides_all + later_heads
    tail_left = left_spike[:, inner_lines - 1 :, :]
    head_left = left_spike[:, :1, :]
    head_right = right_spike[:, :1, :]
    tail_right = right_spike[:, inner_lines - 1 :, :]
    chain_index = lax.broadcasted_iota(jnp.int32, (fields, groups, span_x), 1)
    last_row = chain_index == groups - 1
    chain_mid = jnp.where(last_row, center + 1.0 - tail_right, center - tail_right - head_left)
    chain_low = jnp.where(chain_index > 0, -tail_left, 0.0)
    chain_up = jnp.where(last_row, 0.0, -head_right)
    (separators,) = cyclic_solve(chain_low, chain_mid, chain_up, (chain_side,))
    position = lax.axis_index(("gx", "gy"))
    own_value = lax.dynamic_slice_in_dim(separators, position, 1, axis=1)
    padded_chain = jnp.concatenate([jnp.zeros_like(separators[:, :1, :]), separators], axis=1)
    before = lax.dynamic_slice_in_dim(padded_chain, position, 1, axis=1)
    interior = base_part + before * left_spike + own_value * right_spike
    kept_values = jnp.concatenate([interior, own_value], axis=1)
    return (kept_values, before)


def on_device(source, screening):
    groups = lax.axis_size(("gx", "gy"))
    fields, x_rows, width_y = source.shape
    span_x = x_rows * groups
    block_y = width_y // groups
    kept_lines = block_y // 2
    transform = sine_table(span_x)
    factor = diagonal_factor(screening, span_x)[:, None, :]
    center = factor * factor - 2.0
    columns = to_lines(source)
    spectrum = jnp.einsum("fiy,ki->fyk", columns, transform, precision=HIGHEST)
    paired = spectrum.reshape(fields, kept_lines, 2, span_x)
    even_lines = paired[:, :, 0, :]
    odd_lines = paired[:, :, 1, :]
    following = shifted(even_lines[:, :1, :], ("gx", "gy"), -1)
    later_even = jnp.concatenate([even_lines[:, 1:, :], following], axis=1)
    reduced = even_lines + factor * odd_lines + later_even
    kept_values, before = solve_lines(reduced, center)
    earlier_odd = jnp.concatenate([before, kept_values[:, : kept_lines - 1, :]], axis=1)
    even_values = (even_lines + earlier_odd + kept_values) / factor
    merged = jnp.stack([even_values, kept_values], axis=2).reshape(fields, block_y, span_x)
    solved = jnp.einsum("fyk,ki->fiy", merged, transform, precision=HIGHEST)
    return to_rows(solved)


def solution(mesh):
    return jax.shard_map(
        on_device,
        mesh=mesh,
        in_specs=(P("af", ("gx", "gy"), None), P("af")),
        out_specs=P("af", ("gx", "gy"), None),
        check_vma=False,
    )
```

profile of v0, /device:TPU:0, one launch (start us, length us, event | category | flops | bytes accessed | tf_op | source)
XLA Modules:
  0.0 419.2 jit_solution(3652134350613979381)
XLA Ops:
  0.0 6.0 %copy.11 = f32[1,256,2048]{1,0,2:T(1,128)} copy(f32[1,256,2048]{2,1,0:T(8,128)} %param.2) | data formatting | bytes 4194304 | tf_op args[0]
  6.0 5.2 %all-to-all-start = ((f32[1,256,2048]{1,0,2:T(1,128)}), f32[1,256,2048]{1,0,2:T(1,128)S(1)}, u32[]{:S(2)}, u32[]{:S(2)}) async-start(f32[1,256,2048]{1,0,2:T(1,128)} %copy.11), calls=%async_computation | async-start | bytes 4194304 | tf_op jit(solution)/shard_map/all_to_all | solution.py:66
  11.3 65.9 %fusion.101 = f32[2048,2048]{1,0:T(8,128)} fusion(s32[2048]{0:T(1024)S(1)} %iota_add_fusion), kind=kLoop, calls=%fused_computation.4.clone.1.clone.clone.clone.1 | loop fusion | flops 41943040 | bytes 16785408 | tf_op jit(solution)/shard_map/fiy,ki->fyk/dot_general | solution.py:126
  78.1 65.8 %fusion.103 = f32[2048,2048]{1,0:T(8,128)} fusion(s32[2048]{0:T(1024)S(1)} %iota_add_fusion), kind=kLoop, calls=%fused_computation.4.clone.clone.clone.clone.1 | loop fusion | flops 41943040 | bytes 16785408 | tf_op jit(solution)/shard_map/fyk,ki->fiy/dot_general | solution.py:137
  144.0 1.5 copy.17
  145.4 1.9 copy.12
  147.3 18.8 %fusion.23 = f32[256,2048]{1,0:T(8,128)} fusion(f32[2048,256]{1,0:T(8,128)S(1)} %bitcast.46, f32[2048,2048]{1,0:T(8,128)} %fusion.101), kind=kOutput, calls=%fused_computation.23 | convolution fusion | flops 12884901888 | bytes 20971520 | tf_op jit(solution)/shard_map/fiy,ki->fyk/dot_general | solution.py:126
  166.2 3.7 reshape.360
  170.1 1.3 collective-permute-start
  171.8 1.4 collective-permute-done
  173.1 2.6 fusion.31
  177.4 5.2 %fusion.34 = (f32[1,127,2048]{2,0,1:T(1,128)S(1)}, f32[1,127,2048]{2,0,1:T(1,128)S(1)}, f32[1,127,2048]{2,0,1:T(1,128)S(1)}) fusion(f32[1,128,2048]{2,0,1:T(1,128)S(1)} %fusion.31, f32[1,126,2048]{2,0,1:T(1,128)S(1)} %get-tuple-element.85, f32[1,126,2048]{2,0,1:T(1,128)S(1)} %get-tuple-element.84, f32[1,126,2048]{2,0,1:T(1,128)S(1)} %slice.365, ...), kind=kLoop, calls=%fused_computation.35 | loop fusion | flops 1560576 | bytes 7259128 | tf_op jit(solution)/shard_map/sub | solution.py:54
  182.6 1.6 multiply_subtract_fusion.23
  184.2 1.3 fusion.77
  186.6 9.0 %multiply_subtract_fusion.5 = (f32[1,127,2048]{2,0,1:T(1,128)S(1)}, f32[1,127,2048]{2,0,1:T(1,128)S(1)}, f32[1,127,2048]{2,0,1:T(1,128)S(1)}, f32[1,127,2048]{2,...) fusion(f32[1,127,2048]{2,0,1:T(1,128)S(1)} %get-tuple-element.43, ...), kind=kLoop, calls=%fused_computation.43 | loop fusion | flops 4681728 | bytes 14503904 | tf_op jit(solution)/shard_map/sub | solution.py:54
  195.6 1.3 fusion.73
  197.0 1.3 fusion.75
  198.3 4.1 multiply_subtract_fusion.21
  202.5 1.3 fusion.74
  207.0 10.7 %multiply_subtract_fusion.4 = (f32[1,127,2048]{2,0,1:T(1,128)S(1)}, f32[1,127,2048]{2,0,1:T(1,128)S(1)}, f32[1,127,2048]{2,0,1:T(1,128)S(1)}, f32[1,127,2048]{2,...) fusion(f32[1,127,2048]{2,0,1:T(1,128)S(1)} %get-tuple-element.80, ...), kind=kLoop, calls=%fused_computation.42 | loop fusion | flops 4681728 | bytes 22659072 | tf_op jit(solution)/shard_map/sub | solution.py:54
  217.7 1.4 fusion.69
  219.1 1.3 fusion.71
  220.4 3.8 multiply_subtract_fusion.19
  224.2 1.3 fusion.70
  227.8 1.3 fusion.72
  229.1 10.9 %multiply_subtract_fusion.3 = (f32[1,127,2048]{2,0,1:T(1,128)S(1)}, f32[1,127,2048]{2,0,1:T(1,128)S(1)}, f32[1,127,2048]{2,0,1:T(1,128)S(1)}, f32[1,127,2048]{2,...) fusion(f32[1,127,2048]{2,0,1:T(1,128)S(1)} %get-tuple-element.73, ...), kind=kLoop, calls=%fused_computation.41 | loop fusion | flops 4681728 | bytes 22429696 | tf_op jit(solution)/shard_map/sub | solution.py:54
  240.0 1.3 fusion.65
  242.5 4.1 multiply_subtract_fusion.17
  246.6 1.2 fusion.66
  249.0 1.2 fusion.47
  251.4 11.7 %multiply_subtract_fusion.2 = (f32[1,127,2048]{2,0,1:T(1,128)S(1)}, f32[1,127,2048]{2,0,1:T(1,128)S(1)}, f32[1,127,2048]{2,0,1:T(1,128)S(1)}, f32[1,127,2048]{2,...) fusion(f32[1,127,2048]{2,0,1:T(1,128)S(1)} %get-tuple-element.66, ...), kind=kLoop, calls=%fused_computation.40 | loop fusion | flops 4681728 | bytes 21970944 | tf_op jit(solution)/shard_map/sub | solution.py:54
  263.1 1.2 fusion.61
  265.5 3.8 multiply_subtract_fusion.15
  273.7 11.8 %multiply_subtract_fusion.1 = (f32[1,127,2048]{2,0,1:T(1,128)S(1)}, f32[1,127,2048]{2,0,1:T(1,128)S(1)}, f32[1,127,2048]{2,0,1:T(1,128)S(1)}, f32[1,127,2048]{2,...) fusion(f32[1,127,2048]{2,0,1:T(1,128)S(1)} %get-tuple-element.59, ...), kind=kLoop, calls=%fused_computation.39 | loop fusion | flops 4681728 | bytes 21053440 | tf_op jit(solution)/shard_map/sub | solution.py:54
  289.7 9.3 %multiply_subtract_fusion = (f32[1,127,2048]{2,0,1:T(1,128)S(1)}, f32[1,127,2048]{2,0,1:T(1,128)S(1)}, f32[1,127,2048]{2,0,1:T(1,128)S(1)}, f32[1,127,2048]{2,0,1:T(1,128)S(1)}, f32[1,127,2048]{2,0,1:T(1,128)S(1)}) fusion(f32[1,127,2048]{2,0,1:T(1,128)S(1)} %get-tuple-element.52, f32[1,95,2048]{2,0,1:T(1,128)S(1)} %get-tuple-element.95, ...), kind=kLoop, calls=%fused_computation.38 | loop fusion | flops 4161536 | bytes 16629760 | tf_op jit(solution)/shard_map/sub | solution.py:54
  299.4 5.5 %subtract_divide_fusion.2 = (f32[1,127,2048]{2,0,1:T(1,128)S(1)}, f32[1,127,2048]{2,0,1:T(1,128)S(1)}, f32[1,127,2048]{2,0,1:T(1,128)S(1)}) fusion(f32[1,63,2048]{2,0,1:T(1,128)S(1)} %get-tuple-element.125, f32[1,127,2048]{2,0,1:T(1,128)S(1)} %get-tuple-element.51, f32[1,63,2048]{2,0,1:T(1,128)S(1)} %get-tuple-element.124, f32[1,63,2048]{2,0,1:T(1,128)S(1)} %slice.528, ...), kind=kLoop, calls=%fused_computation.52 | loop fusion | flops 2861056 | bytes 10379264 | tf_op jit(solution)/shard_map/div | solution.py:62
  304.9 5.6 %subtract_divide_fusion = (f32[1,127,2048]{2,0,1:T(1,128)S(1)}, f32[1,127,2048]{2,0,1:T(1,128)S(1)}) fusion(f32[1,127,2048]{2,0,1:T(1,128)S(1)} %get-tuple-element.15, f32[1,63,2048]{2,0,1:T(1,128)S(1)} %get-tuple-element.91, f32[1,127,2048]{2,0,1:T(1,128)S(1)} %get-tuple-element.46, f32[1,127,2048]{2,0,1:T(1,128)S(1)} %get-tuple-element.14, ...), kind=kLoop, calls=%fused_computation.37 | loop fusion | flops 3641344 | bytes 10379264 | tf_op jit(solution)/shard_map/div | solution.py:62
  310.9 11.1 %all_gather.7 = f32[1,8,2048]{2,0,1:T(1,128)S(1)} all-gather(f32[1,1,2048]{2,0,1:T(1,128)S(1)} %get-tuple-element.116), channel_id=1, replica_groups=mesh['af'=4,'gx'=2,'gy'=4] {'gx','gy'}, dimensions={1}, use_global_device_ids=true | all-gather | bytes 73728 | tf_op jit(solution)/shard_map/all_gather | solution.py:91
  322.1 9.2 %all_gather.6 = f32[1,8,2048]{2,0,1:T(1,128)S(1)} all-gather(f32[1,1,2048]{2,0,1:T(1,128)S(1)} %get-tuple-element.117), channel_id=1, replica_groups=mesh['af'=4,'gx'=2,'gy'=4] {'gx','gy'}, dimensions={1}, use_global_device_ids=true | all-gather | bytes 73728 | tf_op jit(solution)/shard_map/all_gather | solution.py:90
  333.3 2.6 multiply_add_fusion
  336.8 3.4 fusion.33
  340.2 6.8 %maximum_reduce_fusion = f32[128,2,2048]{2,1,0:T(2,128)S(1)} fusion(f32[1,128,1,2048]{3,0,2,1:T(1,128)S(1)} %maximum_bitcast_fusion, f32[1,128,1,2048]{3,0,2,1:T(1,128)S(1)} %fusion.33), kind=kLoop, calls=%fused_computation.25 | loop fusion | flops 524288 | bytes 4194304 | tf_op jit(solution)/shard_map/stack | solution.py:136
  347.0 2.4 reshape.359
  349.5 29.4 %fusion.26 = f32[1,2048,256]{2,1,0:T(8,128)S(1)} fusion(f32[256,2048]{1,0:T(8,128)} %reshape.359, f32[2048,2048]{1,0:T(8,128)} %fusion.103), kind=kOutput, calls=%fused_computation.24 | convolution fusion | flops 12884901888 | bytes 20971520 | tf_op jit(solution)/shard_map/fyk,ki->fiy/dot_general | solution.py:137
  378.9 8.6 %copy.15 = f32[1,2048,256]{2,0,1:T(1,128)S(1)} copy(f32[1,2048,256]{2,1,0:T(8,128)S(1)} %fusion.26) | data formatting | bytes 4194304 | tf_op jit(solution)/shard_map/fyk,ki->fiy/transpose | solution.py:137
  387.4 28.6 %all_to_all.33 = f32[1,2048,256]{2,0,1:T(1,128)S(1)} all-to-all(f32[1,2048,256]{2,0,1:T(1,128)S(1)} %copy.15), channel_id=1, replica_groups=mesh['af'=4,'gx'=2,'gy'=4] {'gx','gy'}, dimensions={1} | all-to-all | bytes 4194304 | tf_op jit(solution)/shard_map/all_to_all | solution.py:70
  416.0 1.2 copy.16
  417.2 1.5 all_to_all.30
  (72 shorter events, 25.6 us)
Async XLA Ops:
  6.0 137.9 %all-to-all-start = ((f32[1,256,2048]{1,0,2:T(1,128)}), f32[1,256,2048]{1,0,2:T(1,128)S(1)}, u32[]{:S(2)}, u32[]{:S(2)}) async-start(f32[1,256,2048]{1,0,2:T(1,128)} %copy.11), calls=%async_computation | async-start | bytes 4194304 | tf_op jit(solution)/shard_map/all_to_all | solution.py:66
  170.1 3.1 collective-permute-start
where the time goes:
time: 426 us; the launch traced here: 419 us
  other arithmetic  247 us (58%)
  local copies, waits for them, and re-layouts  65.1 us (15%)
  blocking collectives  48.9 us (11%)
  matrix products  48.2 us (11%)
  starting transfers between devices  6.49 us (2%)
    sub x9, other arithmetic, cyclic_solve(): each_side - left_ratio * shift_rows(each_side, stride, 0.0)  69.4 us
    dot_general x1, other arithmetic, on_device(): spectrum = jnp.einsum('fiy,ki->fyk', columns, transform, precision=HIGHEST)  65.9 us
    dot_general x1, other arithmetic, on_device(): solved = jnp.einsum('fyk,ki->fiy', merged, transform, precision=HIGHEST)  65.8 us
    dot_general x1, matrix products, on_device(): solved = jnp.einsum('fyk,ki->fiy', merged, transform, precision=HIGHEST)  29.4 us
    all_to_all x1, blocking collectives, to_rows(): lax.all_to_all(values, ('gx', 'gy'), split_axis=1, concat_axis=2, tiled=T...  28.6 us
    slice x36, local copies, waits for them, and re-layouts, shift_rows(): values[..., :row_count - offset, :]  24 us
    dot_general x1, matrix products, on_device(): spectrum = jnp.einsum('fiy,ki->fyk', columns, transform, precision=HIGHEST)  18.8 us
    sub x6, other arithmetic, cyclic_solve(): middle - left_ratio * shift_rows(up_band, stride, 0.0)  17.7 us
  transfers between devices with their start and end apart: 2, of which 1 were waited for; matrix products, arithmetic and copies ran while one was open for 32% of the time, Pallas kernels for 0%

commit v1 on v0

v1 whole, which is shorter than its diff:
```python
import functools
import math

import jax
import jax.numpy as jnp
import numpy as np
from jax import lax
from jax.experimental import pallas as pl
from jax.experimental.pallas import tpu as pltpu
from jax.sharding import PartitionSpec as P

LANES = 128
SEGMENTS = 8
TILE = 256
STEP = 32
GRID_AXES = ("gx", "gy")


def mode_numbers(length):
    half = length // 2
    numbers = np.arange(half, dtype=np.int64) + 1
    return np.concatenate([2 * numbers, length + 1 - 2 * numbers])


def double_cosines(length):
    angles = mode_numbers(length).astype(np.float32) * np.float32(math.pi / (length + 1))
    return (np.float32(2.0) * np.cos(angles.astype(np.float64)).astype(np.float32))[None, :]


def angle_tables(length):
    half = length // 2
    columns = np.arange(half, dtype=np.int64)[None, :] + 1
    coarse = np.arange(half // STEP, dtype=np.int64)[:, None] * STEP
    fine = np.arange(STEP, dtype=np.int64)[:, None] + 1
    scale = math.sqrt(2.0 / (length + 1))
    angle = lambda rows: 2.0 * math.pi * (rows * columns % (length + 1)) / (length + 1)
    tables = (
        scale * np.sin(angle(coarse)),
        scale * np.cos(angle(coarse)),
        np.sin(angle(fine)),
        np.cos(angle(fine)),
    )
    return tuple(table.astype(np.float32) for table in tables)


def power(base, exponent):
    result = None
    while exponent:
        if exponent & 1:
            result = base if result is None else result * base
        exponent >>= 1
        if exponent:
            base = base * base
    return result


def decay_of(screening, cosines):
    factor = (4.0 + screening) - cosines
    excess = factor - 2.0
    root = jnp.sqrt(excess * (excess + 4.0))
    return 2.0 / (factor + root), root


def split(values):
    high = values.astype(jnp.bfloat16)
    return high, (values - high.astype(jnp.float32)).astype(jnp.bfloat16)


def mirrored(values):
    lanes = lax.broadcasted_iota(jnp.int32, values.shape, 1)
    return jnp.take_along_axis(values, LANES - 1 - lanes, axis=1)


def parity(shape):
    lanes = lax.broadcasted_iota(jnp.int32, shape, 1)
    return jnp.where(lanes % 2 == 0, 1.0, -1.0)


def table_tile(tables, table_high, table_low, columns):
    coarse_sin, coarse_cos, fine_sin, fine_cos = tables
    for a in range(coarse_sin.shape[0]):
        values = (
            coarse_sin[a : a + 1, columns] * fine_cos[:, columns]
            + coarse_cos[a : a + 1, columns] * fine_sin[:, columns]
        )
        high, low = split(values)
        table_high[a * STEP : (a + 1) * STEP, columns] = high
        table_low[a * STEP : (a + 1) * STEP, columns] = low


def product(high, low, table_high, table_low, columns):
    dot = functools.partial(jnp.dot, preferred_element_type=jnp.float32)
    return (
        dot(high[...], table_high[:, columns])
        + dot(low[...], table_high[:, columns])
        + dot(high[...], table_low[:, columns])
    )


def forward_kernel(
    source, screening, cosines, coarse_sin, coarse_cos, fine_sin, fine_cos,
    spectrum, left_parts, right_parts, moments,
    high, low, table_high, table_low, stage, arrived,
):
    tables = (coarse_sin, coarse_cos, fine_sin, fine_cos)
    rows, length = source.shape
    blocks = length // LANES
    copies = [
        pltpu.make_async_copy(source.at[:, pl.ds(c * LANES, LANES)], stage.at[c], arrived.at[c])
        for c in range(blocks)
    ]
    for copy in copies:
        copy.start()
    half = length // 2
    steps = rows // SEGMENTS
    signs = parity((2 * SEGMENTS, LANES))
    for copy in copies:
        copy.wait()
    for c in range(blocks // 2):
        columns = pl.ds(c * LANES, LANES)
        for g in range(0, steps, 2):
            place = pl.ds(g * SEGMENTS, 2 * SEGMENTS)
            place_sum = pl.ds(rows + g * SEGMENTS, 2 * SEGMENTS)

            def load(column):
                pair = [stage[column, pl.ds(g + e, SEGMENTS, stride=steps), :] for e in range(2)]
                return jnp.concatenate(pair, axis=0)

            near = load(c)
            far = mirrored(load(blocks - 1 - c))
            high[place, columns], low[place, columns] = split(near - far)
            high[place_sum, columns], low[place_sum, columns] = split((near + far) * signs)
    for t in range(half // TILE):
        columns = pl.ds(t * TILE, TILE)
        table_tile(tables, table_high, table_low, columns)
        values = product(high, low, table_high, table_low, columns)
        spectrum[:, t * TILE : (t + 1) * TILE] = values[:rows]
        spectrum[:, half + t * TILE : half + (t + 1) * TILE] = values[rows:]
    decay, _ = decay_of(screening[0], cosines[...])
    stride = power(decay, steps)
    for t in range(length // TILE):
        columns = slice(t * TILE, (t + 1) * TILE)
        ratio = jnp.broadcast_to(decay[:, columns], (SEGMENTS, TILE))
        left = right = jnp.zeros((SEGMENTS, TILE), jnp.float32)
        for g in range(steps):
            mirror = steps - 1 - g
            left = ratio * left + spectrum[g * SEGMENTS : (g + 1) * SEGMENTS, columns]
            right = ratio * right + spectrum[mirror * SEGMENTS : (mirror + 1) * SEGMENTS, columns]
        left_parts[:, columns] = left
        right_parts[:, columns] = right
    left = right = jnp.zeros((1, length), jnp.float32)
    for s in range(SEGMENTS):
        left = stride * left + left_parts[s : s + 1, :]
        right = stride * right + right_parts[SEGMENTS - 1 - s : SEGMENTS - s, :]
    moments[0:1, :] = left
    moments[1:2, :] = right


def backward_kernel(
    groups, spectrum, left_parts, right_parts, all_moments, screening, cosines,
    coarse_sin, coarse_cos, fine_sin, fine_cos,
    solved, high, low, table_high, table_low, left_states, right_states, stage, stored,
):
    tables = (coarse_sin, coarse_cos, fine_sin, fine_cos)
    rows, length = spectrum.shape
    half = length // 2
    steps = rows // SEGMENTS
    position = lax.axis_index(GRID_AXES)
    decay, root = decay_of(screening[0], cosines[...])
    stride = power(decay, steps)
    block = power(decay, rows)
    whole = power(decay, rows * groups + 1)
    left_total = right_total = jnp.zeros((1, length), jnp.float32)
    for d in range(groups):
        left_total = block * left_total + all_moments[2 * d : 2 * d + 1, :]
        e = groups - 1 - d
        right_total = block * right_total + all_moments[2 * e + 1 : 2 * e + 2, :]
    edge = -decay / (1.0 - whole * whole)
    left_state = edge * (right_total - whole * left_total)
    right_state = edge * (left_total - whole * right_total)
    left_own, right_own = left_state, right_state
    for d in range(groups):
        left_own = jnp.where(d == position, left_state, left_own)
        left_state = block * left_state + all_moments[2 * d : 2 * d + 1, :]
        e = groups - 1 - d
        right_own = jnp.where(e == position, right_state, right_own)
        right_state = block * right_state + all_moments[2 * e + 1 : 2 * e + 2, :]
    after_states = []
    for s in range(SEGMENTS):
        left_states[s : s + 1, :] = left_own
        left_own = stride * left_own + left_parts[s : s + 1, :]
        after_states.append(left_own)
    for s in reversed(range(SEGMENTS)):
        right_states[s : s + 1, :] = (right_own + decay * after_states[s]) / root
        right_own = stride * right_own + right_parts[s : s + 1, :]
    for t in range(length // TILE):
        columns = slice(t * TILE, (t + 1) * TILE)
        ratio = jnp.broadcast_to(decay[:, columns], (SEGMENTS, TILE))
        state = left_states[:, columns]
        sums = []
        for g in range(steps):
            state = ratio * state + spectrum[g * SEGMENTS : (g + 1) * SEGMENTS, columns]
            sums.append(state)
        state = right_states[:, columns]
        first = rows * (t * TILE // half)
        inner = slice(t * TILE % half, t * TILE % half + TILE)
        for g in reversed(range(0, steps, 2)):
            later = ratio * (state + sums[g + 1])
            state = ratio * (later + sums[g])
            place = pl.ds(first + g * SEGMENTS, 2 * SEGMENTS)
            high[place, inner], low[place, inner] = split(jnp.concatenate([state, later], axis=0))
    signs = parity((SEGMENTS, LANES))
    blocks = length // LANES
    copies = []
    for t in range(half // TILE):
        table_tile(tables, table_high, table_low, pl.ds(t * TILE, TILE))
        values = product(high, low, table_high, table_low, pl.ds(t * TILE, TILE))
        for c in range(TILE // LANES):
            near = t * TILE // LANES + c
            far = blocks - 1 - near
            columns = slice(c * LANES, (c + 1) * LANES)
            for g in range(steps):
                place = pl.ds(g, SEGMENTS, stride=steps)
                odd = values[g * SEGMENTS : (g + 1) * SEGMENTS, columns]
                even = values[rows + g * SEGMENTS : rows + (g + 1) * SEGMENTS, columns] * signs
                stage[near, place, :] = even + odd
                stage[far, place, :] = mirrored(even - odd)
            for block_index in (near, far):
                target = solved.at[:, pl.ds(block_index * LANES, LANES)]
                copy = pltpu.make_async_copy(stage.at[block_index], target, stored.at[block_index])
                copy.start()
                copies.append(copy)
    for copy in copies:
        copy.wait()


def on_device(source, screening):
    groups = lax.axis_size(GRID_AXES)
    fields, rows, length = source.shape
    half = length // 2
    tables = [jnp.asarray(table) for table in angle_tables(length)]
    cosines = jnp.asarray(double_cosines(length))
    vmem = pl.BlockSpec(memory_space=pltpu.VMEM)
    smem = pl.BlockSpec(memory_space=pltpu.SMEM)
    f32 = lambda *shape: jax.ShapeDtypeStruct(shape, jnp.float32)
    scratch = [
        pltpu.VMEM((2 * rows, half), jnp.bfloat16),
        pltpu.VMEM((2 * rows, half), jnp.bfloat16),
        pltpu.VMEM((half, half), jnp.bfloat16),
        pltpu.VMEM((half, half), jnp.bfloat16),
    ]
    staging = [
        pltpu.VMEM((length // LANES, rows, LANES), jnp.float32),
        pltpu.SemaphoreType.DMA((length // LANES,)),
    ]
    hbm = pl.BlockSpec(memory_space=pl.ANY)
    parts = (SEGMENTS, length)
    params = pltpu.CompilerParams(vmem_limit_bytes=40 * 2**20)

    def one_field(grid, constant):
        spectrum, left_parts, right_parts, moments = pl.pallas_call(
            forward_kernel,
            out_shape=[f32(rows, length), f32(*parts), f32(*parts), f32(2, length)],
            in_specs=[hbm, smem] + [vmem] * 5,
            out_specs=[vmem] * 4,
            scratch_shapes=scratch + staging,
            compiler_params=params,
            name="forward",
        )(grid, constant, cosines, *tables)
        all_moments = lax.all_gather(moments, GRID_AXES, axis=0, tiled=True)
        return pl.pallas_call(
            functools.partial(backward_kernel, groups),
            out_shape=f32(rows, length),
            in_specs=[vmem] * 4 + [smem] + [vmem] * 5,
            out_specs=hbm,
            scratch_shapes=scratch + [pltpu.VMEM(parts, jnp.float32)] * 2 + staging,
            compiler_params=params,
            name="backward",
        )(spectrum, left_parts, right_parts, all_moments, constant, cosines, *tables)

    return jnp.stack([one_field(source[f], screening[f : f + 1]) for f in range(fields)])


def solution(mesh):
    return jax.shard_map(
        on_device,
        mesh=mesh,
        in_specs=(P("af", GRID_AXES, None), P("af")),
        out_specs=P("af", GRID_AXES, None),
        check_vma=False,
    )
```

time: 426 us -> 29.9 us (0.07); the launches traced: 419 us -> 29.6 us
  other arithmetic: 247 us -> 0 us
  local copies, waits for them, and re-layouts: 65.1 us -> 6 us
  matrix products: 48.2 us -> 0 us
  blocking collectives: 48.9 us -> 10.7 us
  Pallas kernels: 0 us -> 12.1 us
  starting transfers between devices: 6.49 us -> 0 us
    dot_general x2 -> x0, other arithmetic: 132 us -> none  [the longest x1 65.9 us: on_device(): spectrum = jnp.einsum('fiy,ki->fyk', columns, transform, precision=HIGHEST)]
    sub x16 -> x0, other arithmetic: 87.1 us -> none  [the longest x9 69.4 us: cyclic_solve(): each_side - left_ratio * shift_rows(each_side, stride, 0.0)]
    dot_general x2 -> x0, matrix products: 48.2 us -> none  [the longest x1 29.4 us: on_device(): solved = jnp.einsum('fyk,ki->fiy', merged, transform, precision=HIGHEST)]
    slice x57 -> x0, local copies, waits for them, and re-layouts: 37.8 us -> none  [the longest x36 24 us: shift_rows(): values[..., :row_count - offset, :]]
    all_to_all x1 -> x0, blocking collectives: 28.6 us -> none  [to_rows(): lax.all_to_all(values, ('gx', 'gy'), split_axis=1, concat_axis=2, tiled=T...]
    div x4 -> x0, other arithmetic: 14.7 us -> none  [the longest x3 11.3 us: cyclic_solve(): return tuple((each_side / middle for each_side in all_sides))]
    pallas_call x0 -> x2, Pallas kernels: none -> 12.1 us  [the longest x1 6.62 us: one_field(): pl.pallas_call(functools.partial(backward_kernel, groups), out_shape=f32(...]
    all_gather x2 -> x1, blocking collectives: 20.4 us -> 10.7 us  [one_field(): all_moments = lax.all_gather(moments, GRID_AXES, axis=0, tiled=True)]
  transfers between devices with their start and end apart: 2 -> 0, of which waited for: 1 -> 0; matrix products, arithmetic and copies ran while one was open for 32% -> 0% of each run, Pallas kernels for 0% -> 0%
where the time goes in v1:
time: 29.9 us; the launch traced here: 29.6 us
  Pallas kernels  12.1 us (40%)
  blocking collectives  10.7 us (36%)
  local copies, waits for them, and re-layouts  6 us (20%)
  between operations  0.74 us (2%)
    all_gather x1, blocking collectives, one_field(): all_moments = lax.all_gather(moments, GRID_AXES, axis=0, tiled=True)  10.7 us
    pallas_call x1, Pallas kernels, one_field(): pl.pallas_call(functools.partial(backward_kernel, groups), out_shape=f32(...  6.62 us
    unnamed x23, local copies, waits for them, and re-layouts  6 us
    pallas_call x1, Pallas kernels, one_field(): pl.pallas_call(forward_kernel, out_shape=[f32(rows, length), f32(*parts),...  5.51 us

profile of v1, /device:TPU:0, one launch (start us, length us, event | category | flops | bytes accessed | tf_op | source)
XLA Modules:
  0.0 29.6 jit_solution(4539499890671235632)
XLA Ops:
  0.0 0.0 copy-start.10
  0.7 0.0 copy-start
  0.7 1.6 %copy-done = f32[1,256,2048]{2,1,0:T(8,128)S(1)} copy-done((f32[1,256,2048]{2,1,0:T(8,128)S(1)}, f32[1,256,2048]{2,1,0:T(8,128)}, u32[]{:S(2)}) %copy-start) | copy-done | bytes 2097176
  2.3 0.0 copy-start.1
  2.3 0.9 %copy-done.1 = f32[32,1024]{1,0:T(8,128)S(1)} copy-done((f32[32,1024]{1,0:T(8,128)S(1)}, f32[32,1024]{1,0:T(8,128)}, u32[]{:S(2)}) %copy-start.1) | copy-done | bytes 131096
  3.2 0.0 copy-start.3
  3.2 0.9 %copy-done.3 = f32[32,1024]{1,0:T(8,128)S(1)} copy-done((f32[32,1024]{1,0:T(8,128)S(1)}, f32[32,1024]{1,0:T(8,128)}, u32[]{:S(2)}) %copy-start.3) | copy-done | bytes 131096
  4.1 0.0 copy-start.5
  4.1 0.9 %copy-done.5 = f32[32,1024]{1,0:T(8,128)S(1)} copy-done((f32[32,1024]{1,0:T(8,128)S(1)}, f32[32,1024]{1,0:T(8,128)}, u32[]{:S(2)}) %copy-start.5) | copy-done | bytes 131096
  5.0 0.0 copy-start.7
  5.0 0.9 %copy-done.7 = f32[32,1024]{1,0:T(8,128)S(1)} copy-done((f32[32,1024]{1,0:T(8,128)S(1)}, f32[32,1024]{1,0:T(8,128)}, u32[]{:S(2)}) %copy-start.7) | copy-done | bytes 131096
  5.9 0.0 copy-start.9
  5.9 0.7 %copy-done.9 = f32[1,2048]{1,0:T(1,128)S(1)} copy-done((f32[1,2048]{1,0:T(1,128)S(1)}, f32[1,2048]{1,0:T(1,128)}, u32[]{:S(2)}) %copy-start.9) | copy-done | bytes 8216
  6.6 0.0 copy-start.2
  6.6 0.0 copy-start.4
  6.6 0.0 copy-start.6
  6.6 0.0 copy-start.8
  6.6 5.5 %forward.1 = (f32[256,2048]{1,0:T(8,128)S(1)}, f32[8,2048]{1,0:T(8,128)S(1)}, f32[8,2048]{1,0:T(8,128)S(1)}, f32[2,2048]{1,0:T(2,128)S(1)}) custom-call(f32[256,2048]{1,0:T(8,128)S(1)} %bitcast.3, f32[1]{0:T(128)S(6)} %copy.8.screening, f32[1,2048]{1,0:T(1,128)S(1)} %copy-done.9, f32[32,1024]{1,0:T(8,128)S(1)} %copy-done.7, f32[32,1024]{1,0:T(8,128)S(1)} %copy-done.5, ...), custom_call_target="tpu_custom_call" | custom-call | tf_op jit(solution)/shard_map/forward/pallas_call | solution.py:261
  12.1 10.7 %all-gather = f32[8,2,2048]{2,1,0:T(2,128)S(1)} all-gather(f32[1,2,2048]{2,1,0:T(2,128)S(1)} %bitcast.4), channel_id=1, replica_groups=mesh['af'=4,'gx'=2,'gy'=4] {'gx','gy'}, dimensions={0}, use_global_device_ids=true | all-gather | bytes 147456 | tf_op jit(solution)/shard_map/all_gather | solution.py:270
  22.8 0.1 reshape.1.all_moments
  22.9 0.0 copy-done.10
  22.9 0.0 copy-done.2
  22.9 0.0 copy-done.4
  22.9 0.0 copy-done.6
  22.9 0.0 copy-done.8
  22.9 6.6 %backward.1 = f32[256,2048]{1,0:T(8,128)} custom-call(f32[256,2048]{1,0:T(8,128)S(1)} %get-tuple-element.9.spectrum, f32[8,2048]{1,0:T(8,128)S(1)} %get-tuple-element.10.left_parts, f32[8,2048]{1,0:T(8,128)S(1)} %get-tuple-element.11.right_parts, f32[16,2048]{1,0:T(8,128)S(1)} %reshape.1.all_moments, f32[1]{0:T(128)S(6)} %copy.8.screening, ...), custom_call_target="tpu_custom_call" | custom-call | tf_op jit(solution)/shard_map/backward/pallas_call | solution.py:271
Async XLA Ops:
  0.0 22.9 %copy-start.10 = (f32[1,2048]{1,0:T(1,128)S(1)}, f32[1,2048]{1,0:T(1,128)}, u32[]{:S(2)}) copy-start(f32[1,2048]{1,0:T(1,128)} %constant.14.clone.cosines) | copy-start | bytes 24580
  0.7 1.6 %copy-start = (f32[1,256,2048]{2,1,0:T(8,128)S(1)}, f32[1,256,2048]{2,1,0:T(8,128)}, u32[]{:S(2)}) copy-start(f32[1,256,2048]{2,1,0:T(8,128)} %param.7) | copy-start | bytes 6291460
  2.3 0.9 %copy-start.1 = (f32[32,1024]{1,0:T(8,128)S(1)}, f32[32,1024]{1,0:T(8,128)}, u32[]{:S(2)}) copy-start(f32[32,1024]{1,0:T(8,128)} %constant.13.clone.fine_cos) | copy-start | bytes 393220
  3.2 0.9 %copy-start.3 = (f32[32,1024]{1,0:T(8,128)S(1)}, f32[32,1024]{1,0:T(8,128)}, u32[]{:S(2)}) copy-start(f32[32,1024]{1,0:T(8,128)} %constant.12.clone.fine_sin) | copy-start | bytes 393220
  4.1 0.9 %copy-start.5 = (f32[32,1024]{1,0:T(8,128)S(1)}, f32[32,1024]{1,0:T(8,128)}, u32[]{:S(2)}) copy-start(f32[32,1024]{1,0:T(8,128)} %constant.11.clone.coarse_cos) | copy-start | bytes 393220
  5.0 0.9 %copy-start.7 = (f32[32,1024]{1,0:T(8,128)S(1)}, f32[32,1024]{1,0:T(8,128)}, u32[]{:S(2)}) copy-start(f32[32,1024]{1,0:T(8,128)} %constant.10.clone.coarse_sin) | copy-start | bytes 393220
  5.9 0.7 %copy-start.9 = (f32[1,2048]{1,0:T(1,128)S(1)}, f32[1,2048]{1,0:T(1,128)}, u32[]{:S(2)}) copy-start(f32[1,2048]{1,0:T(1,128)} %constant.14.clone.cosines) | copy-start | bytes 24580
  6.6 16.3 %copy-start.2 = (f32[32,1024]{1,0:T(8,128)S(1)}, f32[32,1024]{1,0:T(8,128)}, u32[]{:S(2)}) copy-start(f32[32,1024]{1,0:T(8,128)} %constant.13.clone.fine_cos) | copy-start | bytes 393220
  6.6 16.3 %copy-start.4 = (f32[32,1024]{1,0:T(8,128)S(1)}, f32[32,1024]{1,0:T(8,128)}, u32[]{:S(2)}) copy-start(f32[32,1024]{1,0:T(8,128)} %constant.12.clone.fine_sin) | copy-start | bytes 393220
  6.6 16.3 %copy-start.6 = (f32[32,1024]{1,0:T(8,128)S(1)}, f32[32,1024]{1,0:T(8,128)}, u32[]{:S(2)}) copy-start(f32[32,1024]{1,0:T(8,128)} %constant.11.clone.coarse_cos) | copy-start | bytes 393220
  6.6 16.4 %copy-start.8 = (f32[32,1024]{1,0:T(8,128)S(1)}, f32[32,1024]{1,0:T(8,128)}, u32[]{:S(2)}) copy-start(f32[32,1024]{1,0:T(8,128)} %constant.10.clone.coarse_sin) | copy-start | bytes 393220

commit v2 on v1

--- a/solution.py
+++ b/solution.py
@@ -14,6 +14,7 @@
 TILE = 256
 STEP = 32
 GRID_AXES = ("gx", "gy")
+MESH = pl.DeviceIdType.MESH
 
 
 def mode_numbers(length):
@@ -97,10 +98,16 @@
     )
 
 
+def peer(index):
+    across = lax.axis_size("gy")
+    return {"gx": index // across, "gy": index % across}
+
+
 def forward_kernel(
-    source, screening, cosines, coarse_sin, coarse_cos, fine_sin, fine_cos,
-    spectrum, left_parts, right_parts, moments,
+    groups, source, screening, cosines, coarse_sin, coarse_cos, fine_sin, fine_cos,
+    spectrum, left_parts, right_parts, all_moments,
     high, low, table_high, table_low, stage, arrived,
+    moments, landed, send_sems, recv_sems,
 ):
     tables = (coarse_sin, coarse_cos, fine_sin, fine_cos)
     rows, length = source.shape
@@ -113,6 +120,10 @@
         copy.start()
     half = length // 2
     steps = rows // SEGMENTS
+    position = lax.axis_index(GRID_AXES)
+    barrier = pltpu.get_barrier_semaphore()
+    for d in range(1, groups):
+        pl.semaphore_signal(barrier, inc=1, device_id=peer((position + d) % groups), device_id_type=MESH)
     signs = parity((2 * SEGMENTS, LANES))
     for copy in copies:
         copy.wait()
@@ -154,6 +165,33 @@
         right = stride * right + right_parts[SEGMENTS - 1 - s : SEGMENTS - s, :]
     moments[0:1, :] = left
     moments[1:2, :] = right
+    pl.semaphore_wait(barrier, groups - 1)
+    sends = []
+    for d in range(1, groups):
+        send = pltpu.make_async_remote_copy(
+            src_ref=moments,
+            dst_ref=landed.at[position],
+            send_sem=send_sems.at[d],
+            recv_sem=recv_sems.at[position],
+            device_id=peer((position + d) % groups),
+            device_id_type=MESH,
+        )
+        send.start()
+        sends.append(send)
+    all_moments[position] = moments[...]
+    for d in range(1, groups):
+        origin = (position + groups - d) % groups
+        pltpu.make_async_remote_copy(
+            src_ref=moments,
+            dst_ref=landed.at[origin],
+            send_sem=send_sems.at[d],
+            recv_sem=recv_sems.at[origin],
+            device_id=peer(origin),
+            device_id_type=MESH,
+        ).wait_recv()
+        all_moments[origin] = landed[origin]
+    for send in sends:
+        send.wait_send()
 
 
 def backward_kernel(
@@ -172,19 +210,19 @@
     whole = power(decay, rows * groups + 1)
     left_total = right_total = jnp.zeros((1, length), jnp.float32)
     for d in range(groups):
-        left_total = block * left_total + all_moments[2 * d : 2 * d + 1, :]
+        left_total = block * left_total + all_moments[d, 0:1, :]
         e = groups - 1 - d
-        right_total = block * right_total + all_moments[2 * e + 1 : 2 * e + 2, :]
+        right_total = block * right_total + all_moments[e, 1:2, :]
     edge = -decay / (1.0 - whole * whole)
     left_state = edge * (right_total - whole * left_total)
     right_state = edge * (left_total - whole * right_total)
     left_own, right_own = left_state, right_state
     for d in range(groups):
         left_own = jnp.where(d == position, left_state, left_own)
-        left_state = block * left_state + all_moments[2 * d : 2 * d + 1, :]
+        left_state = block * left_state + all_moments[d, 0:1, :]
         e = groups - 1 - d
         right_own = jnp.where(e == position, right_state, right_own)
-        right_state = block * right_state + all_moments[2 * e + 1 : 2 * e + 2, :]
+        right_state = block * right_state + all_moments[e, 1:2, :]
     after_states = []
     for s in range(SEGMENTS):
         left_states[s : s + 1, :] = left_own
@@ -254,20 +292,27 @@
         pltpu.SemaphoreType.DMA((length // LANES,)),
     ]
     hbm = pl.BlockSpec(memory_space=pl.ANY)
+    exchange = [
+        pltpu.VMEM((2, length), jnp.float32),
+        pltpu.VMEM((groups, 2, length), jnp.float32),
+        pltpu.SemaphoreType.DMA((groups,)),
+        pltpu.SemaphoreType.DMA((groups,)),
+    ]
     parts = (SEGMENTS, length)
     params = pltpu.CompilerParams(vmem_limit_bytes=40 * 2**20)
 
     def one_field(grid, constant):
-        spectrum, left_parts, right_parts, moments = pl.pallas_call(
-            forward_kernel,
-            out_shape=[f32(rows, length), f32(*parts), f32(*parts), f32(2, length)],
+        spectrum, left_parts, right_parts, all_moments = pl.pallas_call(
+            functools.partial(forward_kernel, groups),
+            out_shape=[f32(rows, length), f32(*parts), f32(*parts), f32(groups, 2, length)],
             in_specs=[hbm, smem] + [vmem] * 5,
             out_specs=[vmem] * 4,
-            scratch_shapes=scratch + staging,
-            compiler_params=params,
+            scratch_shapes=scratch + staging + exchange,
+            compiler_params=pltpu.CompilerParams(
+                vmem_limit_bytes=40 * 2**20, collective_id=0, has_side_effects=True
+            ),
             name="forward",
         )(grid, constant, cosines, *tables)
-        all_moments = lax.all_gather(moments, GRID_AXES, axis=0, tiled=True)
         return pl.pallas_call(
             functools.partial(backward_kernel, groups),
             out_shape=f32(rows, length),

time: 29.9 us -> 24.9 us (0.83)
  blocking collectives: 10.7 us -> 0 us
  Pallas kernels: 12.1 us -> 18.1 us
    all_gather x1 -> x0, blocking collectives: 10.7 us -> none  [one_field(): all_moments = lax.all_gather(moments, GRID_AXES, axis=0, tiled=True)]
    pallas_call x1, Pallas kernels: 5.51 us -> 11.4 us  [one_field(): pl.pallas_call(functools.partial(forward_kernel, groups), out_shape=[f32(...]
    unnamed x23 -> x12, local copies, waits for them, and re-layouts: 6 us -> 5.9 us
where the time goes in v2:
time: 24.9 us; the launch traced here: 24.7 us
  Pallas kernels  18.1 us (73%)
  local copies, waits for them, and re-layouts  5.9 us (24%)
  between operations  0.67 us (3%)
    pallas_call x1, Pallas kernels, one_field(): pl.pallas_call(functools.partial(forward_kernel, groups), out_shape=[f32(...  11.4 us
    pallas_call x1, Pallas kernels, one_field(): pl.pallas_call(functools.partial(backward_kernel, groups), out_shape=f32(...  6.65 us
    unnamed x12, local copies, waits for them, and re-layouts  5.9 us

profile of v2, /device:TPU:0, one launch (start us, length us, event | category | flops | bytes accessed | tf_op | source)
XLA Modules:
  0.0 24.7 jit_solution(3068051243039051089)
XLA Ops:
  0.7 0.0 copy-start
  0.7 1.6 %copy-done = f32[1,256,2048]{2,1,0:T(8,128)S(1)} copy-done((f32[1,256,2048]{2,1,0:T(8,128)S(1)}, f32[1,256,2048]{2,1,0:T(8,128)}, u32[]{:S(2)}) %copy-start) | copy-done | bytes 2097176
  2.2 0.0 copy-start.1
  2.2 0.9 %copy-done.1 = f32[32,1024]{1,0:T(8,128)S(1)} copy-done((f32[32,1024]{1,0:T(8,128)S(1)}, f32[32,1024]{1,0:T(8,128)}, u32[]{:S(2)}) %copy-start.1) | copy-done | bytes 131096
  3.1 0.0 copy-start.2
  3.2 0.9 %copy-done.2 = f32[32,1024]{1,0:T(8,128)S(1)} copy-done((f32[32,1024]{1,0:T(8,128)S(1)}, f32[32,1024]{1,0:T(8,128)}, u32[]{:S(2)}) %copy-start.2) | copy-done | bytes 131096
  4.1 0.0 copy-start.3
  4.1 0.9 %copy-done.3 = f32[32,1024]{1,0:T(8,128)S(1)} copy-done((f32[32,1024]{1,0:T(8,128)S(1)}, f32[32,1024]{1,0:T(8,128)}, u32[]{:S(2)}) %copy-start.3) | copy-done | bytes 131096
  5.0 0.0 copy-start.4
  5.0 0.9 %copy-done.4 = f32[32,1024]{1,0:T(8,128)S(1)} copy-done((f32[32,1024]{1,0:T(8,128)S(1)}, f32[32,1024]{1,0:T(8,128)}, u32[]{:S(2)}) %copy-start.4) | copy-done | bytes 131096
  5.9 0.0 copy-start.5
  5.9 0.7 %copy-done.5 = f32[1,2048]{1,0:T(1,128)S(1)} copy-done((f32[1,2048]{1,0:T(1,128)S(1)}, f32[1,2048]{1,0:T(1,128)}, u32[]{:S(2)}) %copy-start.5) | copy-done | bytes 8216
  6.6 11.4 %forward.1 = (f32[256,2048]{1,0:T(8,128)S(1)}, f32[8,2048]{1,0:T(8,128)S(1)}, f32[8,2048]{1,0:T(8,128)S(1)}, f32[8,2,2048]{2,1,0:T(2,128)S(1)}) custom-call(f32[256,2048]{1,0:T(8,128)S(1)} %bitcast.2, f32[1]{0:T(128)S(6)} %copy.8.screening, f32[1,2048]{1,0:T(1,128)S(1)} %copy-done.5, f32[32,1024]{1,0:T(8,128)S(1)} %copy-done.4, f32[32,1024]{1,0:T(8,128)S(1)} %copy-done.3, ...), custom_call_target="tpu_custom_call" | custom-call | tf_op jit(solution)/shard_map/forward/pallas_call | solution.py:305
  18.0 6.6 %backward.1 = f32[256,2048]{1,0:T(8,128)} custom-call(f32[256,2048]{1,0:T(8,128)S(1)} %get-tuple-element.9.spectrum, f32[8,2048]{1,0:T(8,128)S(1)} %get-tuple-element.10.left_parts, f32[8,2048]{1,0:T(8,128)S(1)} %get-tuple-element.11.right_parts, f32[8,2,2048]{2,1,0:T(2,128)S(1)} %get-tuple-element.12.all_moments, f32[1]{0:T(128)S(6)} %copy.8.screening, ...), custom_call_target="tpu_custom_call" | custom-call | tf_op jit(solution)/shard_map/backward/pallas_call | solution.py:316
Async XLA Ops:
  0.7 1.6 %copy-start = (f32[1,256,2048]{2,1,0:T(8,128)S(1)}, f32[1,256,2048]{2,1,0:T(8,128)}, u32[]{:S(2)}) copy-start(f32[1,256,2048]{2,1,0:T(8,128)} %param.7) | copy-start | bytes 6291460
  2.2 0.9 %copy-start.1 = (f32[32,1024]{1,0:T(8,128)S(1)}, f32[32,1024]{1,0:T(8,128)}, u32[]{:S(2)}) copy-start(f32[32,1024]{1,0:T(8,128)} %constant.13.clone.fine_cos) | copy-start | bytes 393220
  3.1 0.9 %copy-start.2 = (f32[32,1024]{1,0:T(8,128)S(1)}, f32[32,1024]{1,0:T(8,128)}, u32[]{:S(2)}) copy-start(f32[32,1024]{1,0:T(8,128)} %constant.12.clone.fine_sin) | copy-start | bytes 393220
  4.1 0.9 %copy-start.3 = (f32[32,1024]{1,0:T(8,128)S(1)}, f32[32,1024]{1,0:T(8,128)}, u32[]{:S(2)}) copy-start(f32[32,1024]{1,0:T(8,128)} %constant.11.clone.coarse_cos) | copy-start | bytes 393220
  5.0 0.9 %copy-start.4 = (f32[32,1024]{1,0:T(8,128)S(1)}, f32[32,1024]{1,0:T(8,128)}, u32[]{:S(2)}) copy-start(f32[32,1024]{1,0:T(8,128)} %constant.10.clone.coarse_sin) | copy-start | bytes 393220
  5.9 0.7 %copy-start.5 = (f32[1,2048]{1,0:T(1,128)S(1)}, f32[1,2048]{1,0:T(1,128)}, u32[]{:S(2)}) copy-start(f32[1,2048]{1,0:T(1,128)} %constant.14.clone.cosines) | copy-start | bytes 24580
